TPU v7x, 32 devices: a whole 2x2x4 slice. The times are simulated.
32 devices in a mesh: snap: 2 (over core), shard: 16 (over z, y, x).
Axes of the slice: x: 2, y: 2, z: 4, core: 2. Of those that a mesh axis runs over, the one named last changes fastest.
Arguments:
- snapshots: float32 [32, 524288], P(('snap', 'shard')), may hold values from -6 to 6
- coefficients: float32 [32], P(('snap', 'shard')), may hold values from -1 to 1
Outputs:
- synthesized: float32 [524288], P('shard')
All inputs are finite; a program needn't handle non-finite values.
Results may differ from a plain program's by a relative error of at most 0.000078.
Values sent between devices are 32-bit elements; how exact they have to be, the bound alone decides.
A program may use at most 64 MiB of HBM per device.

v0:
```python
import jax
import jax.numpy as jnp
from jax import lax
from jax.sharding import PartitionSpec as P


def per_device(snapshots, coefficients):
    partial_value = lax.psum_scatter(
        jnp.sum(coefficients[:, None] * snapshots, axis=0), "shard", scatter_dimension=0, tiled=True
    )
    return lax.psum(partial_value, "snap")


def solution(mesh):
    in_specs = (P(("snap", "shard"), None), P(("snap", "shard")))
    out_specs = P("shard")
    return jax.shard_map(
        per_device, mesh=mesh, in_specs=in_specs, out_specs=out_specs, check_vma=False
    )
```

profile of v0, /device:TPU:0, one launch (start us, length us, event | category | flops | bytes accessed | tf_op | source)
XLA Modules:
  0.0 170.1 jit_solution(14000131802462258670)
XLA Ops:
  6.5 0.0 all-reduce.6.cloned.1.call-start
  7.2 4.4 %broadcast_multiply_fusion = f32[1,524288]{1,0:T(1,128)} fusion(f32[1,524288]{1,0:T(1,128)} %param.2, f32[]{:T(128)} %bitcast.3), kind=kLoop, calls=%fused_computation | loop fusion | flops 524288 | bytes 4194308 | tf_op jit(solution)/shard_map/mul | solution.py:9
  11.6 0.0 copy-start
  11.6 0.0 all-reduce.6.cloned.1.call-update
  11.7 0.0 all-reduce.4.cloned.1.call-start
  11.7 0.6 copy-done
  12.3 0.6 dynamic-slice
  13.5 128.7 %all-reduce.6.cloned.1.call-done = f32[524288]{0:T(1024)} async-done(((f32[524288]{0:T(1024)}), f32[524288]{0:T(1024)}) %all-reduce.6.cloned.1.call-update) | async-done | bytes 2097168
  142.2 1.6 dynamic-slice.1
  143.8 0.0 all-reduce.4.cloned.1.call-update
  143.8 17.9 %all-reduce.4.cloned.1.call-done = f32[32768]{0:T(1024)} async-done(((f32[32768]{0:T(1024)}), f32[32768]{0:T(1024)}) %all-reduce.4.cloned.1.call-update) | async-done | bytes 131088 | tf_op jit(solution)/shard_map/psum | solution.py:11
  161.7 1.6 copy.6
Async XLA Ops:
  6.5 135.6 %all-reduce.6.cloned.1.call-start = ((), (), s32[]{:S(2)}) async-start(), calls=%async_computation.1 | async-start | bytes 4194304
  11.6 0.7 copy-start
  11.7 150.0 %all-reduce.4.cloned.1.call-start = ((), (), s32[]{:S(2)}) async-start(), calls=%async_computation | async-start | bytes 262144 | tf_op jit(solution)/shard_map/psum | solution.py:11
Sparse Core Ops, SparseCore 0:
  12.8 129.3 all-reduce.5
  144.5 17.1 all-reduce.3
where the time goes:
time: 170 us
  waiting for transfers between devices  147 us (86%)
  between operations  14.7 us (9%)
  other arithmetic  4.44 us (3%)
  local copies, waits for them, and re-layouts  4.29 us (3%)
    unnamed x3, waiting for transfers between devices  129 us
    psum x1, waiting for transfers between devices, per_device(): return lax.psum(partial_value, 'snap')  17.9 us
    mul x1, other arithmetic, per_device(): coefficients[:, None] * snapshots  4.44 us
    unnamed x5, local copies, waits for them, and re-layouts  4.29 us
  transfers between devices with their start and end apart: 2, of which 2 were waited for; matrix products, arithmetic and copies ran while one was open for 0% of the time, Pallas kernels for 0%

commit v1 on v0

v1 whole, which is shorter than its diff:
```python
import functools

import jax
import jax.numpy as jnp
from jax import lax
from jax.experimental import pallas as pl
from jax.experimental.pallas import tpu as pltpu
from jax.sharding import PartitionSpec as P

MESH = pl.DeviceIdType.MESH
LANES = 128
TILE = 8
CHUNK = 128
PLAN = ((0, 4, 0), (1, 7, 0), (2, 5, 0))


def strides_of(size):
    return tuple(1 << b for b in range(size.bit_length() - 1))


def parts_of(rows, shard_strides):
    tiles = rows // TILE
    whole = sum(share for _, share, _ in PLAN)
    parts, done, seen = [], 0, 0
    for turn, share, wave in PLAN:
        seen += share
        upto = tiles * seen // whole
        if upto > done:
            head = list(shard_strides[:3])
            turn = turn % max(len(head), 1)
            order = head[turn:] + head[:turn] + list(shard_strides[3:])
            parts.append((tuple(order), done * TILE, (upto - done) * TILE, wave))
        done = upto
    return tuple(parts)


def kernel(parts, n, m, coef, snap, out, stage, work, got,
           load_sem, send_sem, recv_sem, share_send, share_recv):
    snap_id = lax.axis_index("snap")
    shard_id = lax.axis_index("shard")
    snap_strides, shard_strides = strides_of(m), strides_of(n)

    def step_of(index, stride):
        return stride - 2 * stride * lax.rem(lax.div(index, stride), 2)

    steps = {("snap", s): step_of(snap_id, s) for s in snap_strides}
    steps.update({("shard", s): step_of(shard_id, s) for s in shard_strides})

    def moved(axis, strides):
        index = snap_id if axis == "snap" else shard_id
        for s in strides:
            index = index + steps[axis, s]
        return index

    def partner(axis, stride):
        if axis == "snap":
            return (moved("snap", (stride,)), shard_id)
        return (snap_id, moved("shard", (stride,)))

    def bits_set(number):
        return tuple(s for s in snap_strides if number & s)

    levels = [
        [("snap", s) for s in snap_strides] + [("shard", s) for s in order]
        for order, _, _, _ in parts
    ]
    depth = len(levels[0])
    blocks = n * m

    loads = []
    for p, (_, first, rows, _) in enumerate(parts):
        load = pltpu.make_async_copy(
            snap.at[:, :, pl.ds(first, rows), :], stage.at[:, :, pl.ds(first, rows), :], load_sem.at[p]
        )
        load.start()
        loads.append(load)

    barrier = pltpu.get_barrier_semaphore()
    peers = [(moved("snap", bits_set(d)), shard_id) for d in range(1, m)]
    peers += [partner("shard", s) for s in shard_strides]
    for peer in peers:
        pl.semaphore_signal(barrier, inc=1, device_id=peer, device_id_type=MESH)

    scale = coef[0]
    sends = []

    def copy_of(p, level):
        _, first, rows, _ = parts[p]
        half = (blocks >> (level + 1)) * rows
        span = pl.ds(blocks * first + half, half)
        return pltpu.make_async_remote_copy(
            src_ref=work.at[span, :],
            dst_ref=got.at[span, :],
            send_sem=send_sem.at[p * depth + level],
            recv_sem=recv_sem.at[p * depth + level],
            device_id=partner(*levels[p][level]),
            device_id_type=MESH,
        )

    copies = {(p, level): copy_of(p, level) for p in range(len(parts)) for level in range(depth)}

    def weigh(p, positions):
        _, first, rows, _ = parts[p]
        for position in positions:
            taken = [levels[p][k] for k in range(depth) if (position >> (depth - 1 - k)) & 1]
            owner = moved("shard", [s for axis, s in taken if axis == "shard"])
            part = moved("snap", [s for axis, s in taken if axis == "snap"])
            work[pl.ds(blocks * first + position * rows, rows), :] = (
                scale * stage[owner, part, pl.ds(first, rows), :]
            )

    def accumulate(p, level, upper):
        _, first, rows, _ = parts[p]
        half = (blocks >> (level + 1)) * rows
        quarter = half // 2
        base, source = blocks * first + (quarter if upper else 0), half
        for at in range(0, quarter, CHUNK):
            count = min(CHUNK, quarter - at)
            here = pl.ds(base + at, count)
            there = pl.ds(base + source + at, count)
            work[here, :] = work[here, :] + got[there, :]

    for p in range(len(parts)):
        loads[p].wait()
        weigh(p, range(blocks // 2, blocks))
        if p == 0:
            pl.semaphore_wait(barrier, len(peers))
        copies[p, 0].start()
        weigh(p, range(blocks // 2))

    shares = []
    todo = [(level + parts[p][3], level, p) for level in range(1, depth + 1) for p in range(len(parts))]
    for _, level, p in sorted(todo):
        _, first, rows, _ = parts[p]
        copies[p, level - 1].wait_recv()
        if level < depth:
            accumulate(p, level - 1, True)
            copies[p, level].start()
            accumulate(p, level - 1, False)
        else:
            base = blocks * first
            out[snap_id, pl.ds(first, rows), :] = work[pl.ds(base, rows), :] + got[pl.ds(base + rows, rows), :]
            for d in range(1, m):
                share = pltpu.make_async_remote_copy(
                    src_ref=out.at[snap_id, pl.ds(first, rows), :],
                    dst_ref=out.at[snap_id, pl.ds(first, rows), :],
                    send_sem=share_send.at[p * m + d],
                    recv_sem=share_recv.at[p * m + d],
                    device_id=(moved("snap", bits_set(d)), shard_id),
                    device_id_type=MESH,
                )
                share.start()
                shares.append(share)

    for share in shares:
        share.wait_recv()
    for copy in copies.values():
        copy.wait_send()
    for share in shares:
        share.wait_send()


def by_collectives(snapshots, coefficients):
    total = jnp.sum(coefficients[:, None] * snapshots, axis=0)
    return lax.psum(lax.psum_scatter(total, "shard", scatter_dimension=0, tiled=True), "snap")


def per_device(n, m, snapshots, coefficients):
    count, params = snapshots.shape
    power = n & (n - 1) == 0 and m & (m - 1) == 0 and n * m > 1
    if count != 1 or not power or params % (n * m * TILE * LANES):
        return by_collectives(snapshots, coefficients)
    rows = params // (n * m * LANES)
    parts = parts_of(rows, strides_of(n))
    depth = len(strides_of(n)) + len(strides_of(m))
    result = pl.pallas_call(
        functools.partial(kernel, parts, n, m),
        out_shape=jax.ShapeDtypeStruct((m, rows, LANES), jnp.float32),
        in_specs=[pl.BlockSpec(memory_space=pltpu.SMEM), pl.BlockSpec(memory_space=pl.ANY)],
        out_specs=pl.BlockSpec(memory_space=pltpu.VMEM),
        scratch_shapes=[
            pltpu.VMEM((n, m, rows, LANES), jnp.float32),
            pltpu.VMEM((n * m * rows, LANES), jnp.float32),
            pltpu.VMEM((n * m * rows, LANES), jnp.float32),
            pltpu.SemaphoreType.DMA((len(parts),)),
            pltpu.SemaphoreType.DMA((len(parts) * depth,)),
            pltpu.SemaphoreType.DMA((len(parts) * depth,)),
            pltpu.SemaphoreType.DMA((len(parts) * m,)),
            pltpu.SemaphoreType.DMA((len(parts) * m,)),
        ],
        compiler_params=pltpu.CompilerParams(collective_id=0, has_side_effects=True),
    )(coefficients, snapshots.reshape(n, m, rows, LANES))
    return result.reshape(params // n)


def solution(mesh):
    n, m = mesh.shape["shard"], mesh.shape["snap"]
    return jax.shard_map(
        functools.partial(per_device, n, m),
        mesh=mesh,
        in_specs=(P(("snap", "shard"), None), P(("snap", "shard"))),
        out_specs=P("shard"),
        check_vma=False,
    )
```

time: 170 us -> 30.5 us (0.18)
  waiting for transfers between devices: 147 us -> 0 us
  Pallas kernels: 0 us -> 28.1 us
  between operations: 14.7 us -> 0.66 us
  other arithmetic: 4.44 us -> 0 us
  local copies, waits for them, and re-layouts: 4.29 us -> 1.57 us
    unnamed x3 -> x0, waiting for transfers between devices: 129 us -> none
    pallas_call x0 -> x1, Pallas kernels: none -> 28.1 us  [per_device(): pl.pallas_call(functools.partial(kernel, parts, n, m), out_shape=jax.Shap...]
    psum x1 -> x0, waiting for transfers between devices: 17.9 us -> none  [per_device(): return lax.psum(partial_value, 'snap')]
    mul x1 -> x0, other arithmetic: 4.44 us -> none  [per_device(): coefficients[:, None] * snapshots]
    unnamed x5 -> x1, local copies, waits for them, and re-layouts: 4.29 us -> 1.57 us
  transfers between devices with their start and end apart: 2 -> 0, of which waited for: 2 -> 0; matrix products, arithmetic and copies ran while one was open for 0% -> 0% of each run, Pallas kernels for 0% -> 0%
where the time goes in v1:
time: 30.5 us; the launch traced here: 30.3 us
  Pallas kernels  28.1 us (92%)
  local copies, waits for them, and re-layouts  1.57 us (5%)
  between operations  0.66 us (2%)
    pallas_call x1, Pallas kernels, per_device(): pl.pallas_call(functools.partial(kernel, parts, n, m), out_shape=jax.Shap...  28.1 us
    unnamed x1, local copies, waits for them, and re-layouts  1.57 us

profile of v1, /device:TPU:0, one launch (start us, length us, event | category | flops | bytes accessed | tf_op | source)
XLA Modules:
  0.0 30.3 jit_solution(1638587786592449534)
XLA Ops:
  0.7 28.1 %shard_map.28 = f32[2,128,128]{2,1,0:T(8,128)} custom-call(f32[1]{0:T(128)S(6)} %copy.4.coef, f32[16,2,128,128]{3,2,1,0:T(8,128)} %bitcast.2), custom_call_target="tpu_custom_call" | custom-call | tf_op jit(solution)/shard_map/pallas_call | solution.py:176
  28.8 1.6 %copy.5 = f32[32768]{0:T(1024)} copy(f32[32768]{0:T(1024)} %bitcast.3) | data formatting | bytes 262144

commit v2 on v1

--- a/solution.py
+++ b/solution.py
@@ -11,7 +11,15 @@
 LANES = 128
 TILE = 8
 CHUNK = 128
-PLAN = ((0, 4, 0), (1, 7, 0), (2, 5, 0))
+PLAN = (
+    ((1, 0, 3, 2), 3, (0, 7, 14, 24, 29)),
+    ((0, 3, 1, 2), 3, (1, 8, 19, 25, 31)),
+    ((2, 1, 0, 3), 3, (2, 9, 15, 21, 28)),
+    ((0, 2, 1, 3), 2, (3, 11, 17, 23, 32)),
+    ((2, 0, 3, 1), 2, (4, 12, 18, 27, 34)),
+    ((1, 0, 2, 3), 2, (5, 10, 16, 22, 30)),
+    ((1, 3, 0, 2), 1, (6, 13, 20, 26, 33)),
+)
 
 
 def strides_of(size):
@@ -22,14 +30,13 @@
     tiles = rows // TILE
     whole = sum(share for _, share, _ in PLAN)
     parts, done, seen = [], 0, 0
-    for turn, share, wave in PLAN:
+    for turn, share, ranks in PLAN:
         seen += share
         upto = tiles * seen // whole
         if upto > done:
-            head = list(shard_strides[:3])
-            turn = turn % max(len(head), 1)
-            order = head[turn:] + head[:turn] + list(shard_strides[3:])
-            parts.append((tuple(order), done * TILE, (upto - done) * TILE, wave))
+            order = [shard_strides[b] for b in turn if b < len(shard_strides)]
+            order += shard_strides[len(order):]
+            parts.append((tuple(order), done * TILE, (upto - done) * TILE, ranks))
         done = upto
     return tuple(parts)
 
@@ -69,9 +76,8 @@
 
     loads = []
     for p, (_, first, rows, _) in enumerate(parts):
-        load = pltpu.make_async_copy(
-            snap.at[:, :, pl.ds(first, rows), :], stage.at[:, :, pl.ds(first, rows), :], load_sem.at[p]
-        )
+        span = pl.ds(first, rows)
+        load = pltpu.make_async_copy(snap.at[:, :, span, :], stage.at[:, :, span, :], load_sem.at[p])
         load.start()
         loads.append(load)
 
@@ -129,7 +135,12 @@
         weigh(p, range(blocks // 2))
 
     shares = []
-    todo = [(level + parts[p][3], level, p) for level in range(1, depth + 1) for p in range(len(parts))]
+    extra = depth - len(PLAN[0][2])
+    todo = [
+        (ranks[max(level - 1 - extra, 0)], level, p)
+        for p, (_, _, _, ranks) in enumerate(parts)
+        for level in range(1, depth + 1)
+    ]
     for _, level, p in sorted(todo):
         _, first, rows, _ = parts[p]
         copies[p, level - 1].wait_recv()
@@ -176,7 +187,7 @@
     result = pl.pallas_call(
         functools.partial(kernel, parts, n, m),
         out_shape=jax.ShapeDtypeStruct((m, rows, LANES), jnp.float32),
-        in_specs=[pl.BlockSpec(memory_space=pltpu.SMEM), pl.BlockSpec(memory_space=pl.ANY)],
+        in_specs=[pl.BlockSpec(memory_space=pltpu.SMEM), pl.BlockSpec(memory_space=pltpu.HBM)],
         out_specs=pl.BlockSpec(memory_space=pltpu.VMEM),
         scratch_shapes=[
             pltpu.VMEM((n, m, rows, LANES), jnp.float32),
@@ -188,7 +199,7 @@
             pltpu.SemaphoreType.DMA((len(parts) * m,)),
             pltpu.SemaphoreType.DMA((len(parts) * m,)),
         ],
-        compiler_params=pltpu.CompilerParams(collective_id=0, has_side_effects=True),
+        compiler_params=pltpu.CompilerParams(collective_id=0, has_side_effects=True, vmem_limit_bytes=52 * 1024 * 1024),
     )(coefficients, snapshots.reshape(n, m, rows, LANES))
     return result.reshape(params // n)
 

time: 30.5 us -> 24.6 us (0.81)
  Pallas kernels: 28.1 us -> 23.1 us
  local copies, waits for them, and re-layouts: 1.57 us -> 0.66 us
    pallas_call x1, Pallas kernels: 28.1 us -> 23.1 us  [per_device(): pl.pallas_call(functools.partial(kernel, parts, n, m), out_shape=jax.Shap...]
    unnamed x1, local copies, waits for them, and re-layouts: 1.57 us -> 0.66 us
where the time goes in v2:
time: 24.6 us; the launch traced here: 24.5 us
  Pallas kernels  23.1 us (94%)
  local copies, waits for them, and re-layouts  0.66 us (3%)
  between operations  0.66 us (3%)
    pallas_call x1, Pallas kernels, per_device(): pl.pallas_call(functools.partial(kernel, parts, n, m), out_shape=jax.Shap...  23.1 us
    unnamed x1, local copies, waits for them, and re-layouts  0.66 us

profile of v2, /device:TPU:0, one launch (start us, length us, event | category | flops | bytes accessed | tf_op | source)
XLA Modules:
  0.0 24.5 jit_solution(18207017623009736029)
XLA Ops:
  0.7 23.1 %shard_map.28 = f32[2,128,128]{2,1,0:T(8,128)S(1)} custom-call(f32[1]{0:T(128)S(6)} %copy.4.coef, f32[16,2,128,128]{3,2,1,0:T(8,128)} %bitcast.3), custom_call_target="tpu_custom_call" | custom-call | tf_op jit(solution)/shard_map/pallas_call | solution.py:187
  23.8 0.7 %copy.5 = f32[32768]{0:T(1024)} copy(f32[32768]{0:T(1024)S(1)} %bitcast.2) | data formatting | bytes 262144
